TPU v7x, 32 devices: a whole 2x2x4 slice. The times are simulated.
32 devices in a mesh: gx: 2 (over x), gy: 4 (over y, core), gz: 4 (over z).
Axes of the slice: x: 2, y: 2, z: 4, core: 2. Of those that a mesh axis runs over, the one named last changes fastest.
Arguments:
- metric_pert: float32 [6, 32, 64, 512], P(None, 'gx', 'gy', 'gz'), may hold values from -1.8 to 1.8
- curvature: float32 [6, 32, 64, 512], P(None, 'gx', 'gy', 'gz'), may hold values from -6 to 6
- interp_weights: bfloat16 [2, 4, 32, 64, 4096], P('gx', 'gy', 'gz'), may hold values from -0.09375 to 0.09375
- point_ids: int32 [2, 4, 32, 64], P('gx', 'gy', 'gz'), may hold values from 0 to 6144, as said below
- theta: float32 [6144], replicated, may hold values from 0.05 to 3.09
- phi: float32 [6144], replicated, may hold values from -3.140625 to 3.140625
Outputs:
- psi4_field: bfloat16 [2, 32, 64, 512], P(None, 'gx', 'gy', 'gz')
- modes: float32 [3, 2, 77], replicated
Inputs may be any that keep to these rules, and one draw needn't show every extreme that they name: `point_ids`: the grid is a window of the extraction region that the spheres cross. A live entry names a sphere point; the value 6144 marks an empty slot, and each list holds its live entries first. The points of sphere s lie in the 9 consecutive block layers along the third dimension that begin at layer s * 10; each point belongs to one column (bx, by) and is listed in exactly two blocks of that column that are adjacent along the third dimension. Some block's list is full, every listing block holds at least 32 live entries, and blocks outside these layers list no point.
All inputs are finite; a program needn't handle non-finite values.
Results may differ from a plain program's by a relative error of at most 0.0032.
Values sent between devices are 32-bit elements; how exact they have to be, the bound alone decides.
A program may use at most 64 MiB of HBM per device.

v0:
```python
import functools
import math

import jax
import jax.numpy as jnp
import numpy as np
from jax import lax
from jax.experimental import pallas as pl
from jax.experimental.pallas import tpu as pltpu
from jax.sharding import PartitionSpec as P

BLK = 16
PB = 64
PTS = 2048
SPHERES = 3
LMAX = 8
MODES = (LMAX + 1) ** 2 - 4
ROWS = -(-MODES // 8) * 8
AXES = ("gx", "gy", "gz")
PAIRS = [[0, 1, 2], [1, 3, 4], [2, 4, 5]]
MESH = pl.DeviceIdType.MESH
LO = 8


def build_table():
    table = np.zeros((ROWS, ROWS))
    for degree in range(2, LMAX + 1):
        base = degree * degree - 4
        for order in range(-degree, degree + 1):
            lead = (-1.0) ** order * math.sqrt(
                math.factorial(degree + order)
                * math.factorial(degree - order)
                * (2 * degree + 1)
                / (4.0 * math.pi * math.factorial(degree - 2) * math.factorial(degree + 2))
            )
            for step in range(0, degree + 3):
                lower = step - 2 - order
                if 0 <= lower <= degree - 2:
                    table[base + order + degree, base + 2 * step - 2 - order] += (
                        lead
                        * math.comb(degree + 2, step)
                        * math.comb(degree - 2, lower)
                        * (-1.0) ** (degree - step + 2)
                    )
    return table.astype(np.float32)


def power(bits, base, count):
    result = None
    for bit in range(count):
        factor = jnp.where((bits >> bit) & 1 == 1, base, 1.0)
        result = factor if result is None else result * factor
        base = base * base
    return result


def harmonics(ids, theta_ref, phi_ref, table):
    blocks, slots = ids.shape
    copies = 128 // slots
    wide = jnp.concatenate([ids] * copies, 1)
    safe = jnp.minimum(wide, SPHERES * PTS - 1)
    row, lane = safe >> 7, safe & 127
    theta = jnp.zeros(wide.shape, jnp.float32)
    phi = jnp.zeros(wide.shape, jnp.float32)
    for index in range(theta_ref.shape[0]):
        here = row == index
        one = jnp.broadcast_to(theta_ref[index : index + 1, :], wide.shape)
        theta = jnp.where(here, jnp.take_along_axis(one, lane, axis=1), theta)
        one = jnp.broadcast_to(phi_ref[index : index + 1, :], wide.shape)
        phi = jnp.where(here, jnp.take_along_axis(one, lane, axis=1), phi)

    def flat(array):
        return jnp.concatenate([array[b : b + 1, :slots] for b in range(blocks)], 1)

    half = theta * 0.5
    cosine, sine = flat(jnp.cos(half)), flat(jnp.sin(half))
    re, im = flat(jnp.cos(phi)), flat(jnp.sin(phi))
    sphere = flat(wide // PTS)
    k = lax.broadcasted_iota(jnp.int32, (ROWS, 1), 0)
    degree = jnp.full((ROWS, 1), 2, jnp.int32)
    for below in range(2, LMAX + 1):
        degree = degree + (k >= (below + 1) ** 2 - 4).astype(jnp.int32)
    first = k - (degree * degree - 4)
    order = first - degree
    mono = power(first, cosine, 5) * power(2 * degree - first, sine, 5)
    amplitude = jnp.dot(table, mono, precision=lax.Precision.HIGHEST, preferred_element_type=jnp.float32)
    size = jnp.abs(order)
    total_re = jnp.ones((ROWS, blocks * slots), jnp.float32)
    total_im = jnp.zeros((ROWS, blocks * slots), jnp.float32)
    for bit in range(4):
        on = (size >> bit) & 1 == 1
        f_re, f_im = jnp.where(on, re, 1.0), jnp.where(on, im, 0.0)
        total_re, total_im = total_re * f_re - total_im * f_im, total_re * f_im + total_im * f_re
        re, im = re * re - im * im, 2.0 * re * im
    total_im = jnp.where(order < 0, -total_im, total_im)
    return amplitude * total_re, amplitude * total_im, sphere


def curls(deriv):
    def minus(one, two):
        if two is None:
            return one
        return -two if one is None else one - two

    def plus(one, two):
        if one is None or two is None:
            return two if one is None else one
        return one + two

    def curl(row, col):
        one, two = (row + 1) % 3, (row + 2) % 3
        return minus(deriv(one, PAIRS[two][col]), deriv(two, PAIRS[one][col]))

    magnetic = {}
    for row in range(3):
        magnetic[row, row] = curl(row, row)
        for col in range(row + 1, 3):
            both = plus(curl(row, col), curl(col, row))
            magnetic[row, col] = None if both is None else 0.5 * both
    return magnetic


def contract_frame(electric, magnetic, x, y, z):
    rho2 = x * x + y * y
    rho = jnp.sqrt(rho2)
    radius = jnp.sqrt(rho2 + z * z)
    inv_rho, inv_radius = 1.0 / rho, 1.0 / radius
    cos_phi, sin_phi = x * inv_rho, y * inv_rho
    cos_theta, sin_theta = z * inv_radius, rho * inv_radius
    t = [cos_theta * cos_phi, cos_theta * sin_phi, -sin_theta]
    p = [-sin_phi, cos_phi, None]
    real, imag = 0.0, 0.0
    for row in range(3):
        for col in range(row, 3):
            weight = 0.5 if row == col else 1.0
            plus = t[row] * t[col]
            if col < 2:
                plus = plus - p[row] * p[col]
            plus = plus * weight
            cross = None
            if row < 2:
                cross = p[row] * t[col]
                if col < 2:
                    cross = cross + t[row] * p[col]
                cross = cross * weight
            e, b = electric[row, col], magnetic[row, col]
            real = real + e * plus
            if b is not None:
                imag = imag - b * plus
            if cross is not None:
                imag = imag - e * cross
                if b is not None:
                    real = real - b * cross
    return real, imag


def face_tile(axis, sign, near, far, x, y, z):
    def combine(comp, one, two):
        beside = near(comp)
        value = far(comp) * (-two)
        return value if beside is None else value + beside * one

    electric = {}
    for row in range(3):
        for col in range(row, 3):
            electric[row, col] = combine(PAIRS[row][col], 16.0 / 12.0, 1.0 / 12.0) * -0.5
    deriv = functools.lru_cache(None)(
        lambda along, comp: combine(6 + comp, 8.0 / 12.0, 1.0 / 12.0) * sign if along == axis else None
    )
    return contract_frame(electric, curls(deriv), x, y, z)


def weyl_tile(field, x, y, z):
    lane = lax.broadcasted_iota(jnp.int32, z.shape, 1)
    last = z.shape[1]

    def along(comp, axis, offset):
        if axis == 0:
            return field(comp, offset, 0)
        if axis == 1:
            return field(comp, 0, offset)
        outside = lane < offset if offset > 0 else lane >= last + offset
        return pltpu.roll(jnp.where(outside, 0.0, field(comp, 0, 0)), (-offset) % last, 1)

    def first(comp, axis):
        near = along(comp, axis, 1) - along(comp, axis, -1)
        far = along(comp, axis, 2) - along(comp, axis, -2)
        return near * (8.0 / 12.0) - far * (1.0 / 12.0)

    k = [field(6 + comp, 0, 0) for comp in range(6)]
    trace = k[0] + k[3] + k[5]
    electric = {}
    for row in range(3):
        for col in range(row, 3):
            comp = PAIRS[row][col]
            near, far = 0.0, 0.0
            for axis in range(3):
                near = near + (along(comp, axis, 1) + along(comp, axis, -1))
                far = far + (along(comp, axis, 2) + along(comp, axis, -2))
            laplace = near * (16.0 / 12.0) - far * (1.0 / 12.0) - field(comp, 0, 0) * 7.5
            square = sum(k[PAIRS[row][l]] * k[PAIRS[l][col]] for l in range(3))
            electric[row, col] = trace * k[comp] - square - 0.5 * laplace
    deriv = functools.lru_cache(None)(lambda axis, comp: first(6 + comp, axis))
    return contract_frame(electric, curls(deriv), x, y, z)


def swap_blocks(tile):
    count = tile.shape[0]
    width = tile.shape[1] // count
    rolled = pltpu.roll(tile, 0, 1, stride=width, stride_axis=0)
    row = lax.broadcasted_iota(jnp.int32, tile.shape, 0)
    block = lax.broadcasted_iota(jnp.int32, tile.shape, 1) // width
    mixed = jnp.take_along_axis(rolled, (block - row + count) % count, axis=0)
    out = mixed
    for bit in range(3):
        shift = (1 << bit) * width
        out = jnp.where((row >> bit) & 1 == 1, pltpu.roll(out, tile.shape[1] - shift, 1), out)
    return out


def kernel(
    counts, metric, curvature, weights, ids_hbm, theta_hbm, phi_hbm, table_hbm,
    psi_ref, modes_ref,
    F, W, ids_ref, theta_ref, phi_ref, table_ref, PS, XS, XR, YS, YR, ZS, ZR, RED, MINE,
    load_sem, xs_sem, xr_sem, ys_sem, yr_sem, zs_sem, zr_sem, ps_sem, pr_sem,
):
    cx, cy, cz = psi_ref.shape[1:]
    here = {axis: lax.axis_index(axis) for axis in AXES}
    loads = [
        pltpu.make_async_copy(source, target, load_sem.at[place])
        for place, (source, target) in enumerate((
            (metric, F.at[pl.ds(0, 6), pl.ds(2, cx), pl.ds(LO, cy)]),
            (curvature, F.at[pl.ds(6, 6), pl.ds(2, cx), pl.ds(LO, cy)]),
            (ids_hbm, ids_ref),
            (theta_hbm, theta_ref),
            (phi_hbm, phi_ref),
            (table_hbm, table_ref),
            (weights, W),
        ))
    ]
    for copy in loads:
        copy.start()
    plane = counts["gx"] * counts["gy"]
    rank = here["gx"] * counts["gy"] + here["gy"]

    def in_plane(step):
        other = lax.rem(rank + step, plane)
        return {"gx": other // counts["gy"], "gy": lax.rem(other, counts["gy"])}

    def in_column(step):
        return {"gz": lax.rem(here["gz"] + step, counts["gz"])}

    groups = ((rank, plane, in_plane), (here["gz"], counts["gz"], in_column))
    barrier = pltpu.get_barrier_semaphore()
    for _, count, peer in groups:
        for step in range(1, count):
            pl.semaphore_signal(barrier, inc=1, device_id=peer(step), device_id_type=MESH)

    for edge in (0, cx + 2):
        F[:, edge : edge + 2, LO : LO + cy, :] = jnp.zeros((12, 2, cy, cz), jnp.float32)
    for edge in (LO - 8, LO + cy):
        F[:, 2 : 2 + cx, edge : edge + 8, :] = jnp.zeros((12, cx, 8, cz), jnp.float32)

    def coordinate(axis, cells, index):
        return (here[axis] * cells + index).astype(jnp.float32) + (0.5 - counts[axis] * cells / 2.0)

    loads[0].wait()
    loads[1].wait()
    tile = (8, cz)
    sub = lax.broadcasted_iota(jnp.int32, tile, 0)
    lane = lax.broadcasted_iota(jnp.int32, tile, 1)
    z = coordinate("gz", cz, lane)

    def layers(cells):
        return (
            (0, 0, -2, None, 0), (0, 1, -1, 0, 1),
            (1, 0, cells, cells - 1, cells - 2), (1, 1, cells + 1, None, cells - 1),
        )

    for side, layer, cell, near, far in layers(cx):
        for part in range(cy // 8):
            rows = slice(LO + 8 * part, LO + 8 * part + 8)
            load = lambda at, rows=rows: lambda comp: None if at is None else F[comp, 2 + at, rows, :]
            real, imag = face_tile(
                0, 1.0 - 2.0 * side, load(near), load(far),
                coordinate("gx", cx, jnp.full(tile, cell, jnp.int32)), coordinate("gy", cy, sub + 8 * part), z,
            )
            XS[side, 0, layer, 8 * part : 8 * part + 8, :] = real
            XS[side, 1, layer, 8 * part : 8 * part + 8, :] = imag
    for side, layer, cell, near, far in layers(cy):
        for part in range(cx // 8):
            rows = slice(2 + 8 * part, 2 + 8 * part + 8)
            load = lambda at, rows=rows: lambda comp: None if at is None else F[comp, rows, LO + at, :]
            real, imag = face_tile(
                1, 1.0 - 2.0 * side, load(near), load(far),
                coordinate("gx", cx, sub + 8 * part), coordinate("gy", cy, jnp.full(tile, cell, jnp.int32)), z,
            )
            YS[side, 0, layer, 8 * part : 8 * part + 8, :] = real
            YS[side, 1, layer, 8 * part : 8 * part + 8, :] = imag

    spot_of = ((lane + 2) & (cz - 1)) >> 2
    place = (lane + 2) & 3

    @functools.lru_cache(None)
    def z_edges(comp):
        packed = None
        for part in range(cy // 8):
            for x in range(cx):
                spot = part * cx + x
                moved = F[comp, 2 + x, LO + 8 * part : LO + 8 * part + 8, :]
                if spot:
                    moved = jnp.where(spot_of == spot, pltpu.roll(moved, 4 * spot, 1), packed)
                packed = moved
        return packed

    def z_near(comp):
        edges = z_edges(comp)
        return jnp.where(place == 3, pltpu.roll(edges, 1, 1), jnp.where(place == 0, pltpu.roll(edges, cz - 1, 1), 0.0))

    real, imag = face_tile(
        2, jnp.where(place >= 2, 1.0, -1.0), functools.lru_cache(None)(z_near), z_edges,
        coordinate("gx", cx, spot_of % cx), coordinate("gy", cy, (spot_of // cx) * 8 + sub),
        coordinate("gz", cz, jnp.where(place >= 2, place - 4, cz + place)),
    )
    ZS[0] = real
    ZS[1] = imag

    pl.semaphore_wait(barrier, sum(count - 1 for _, count, _ in groups))

    moves = []
    for axis, send, recv, send_sem, recv_sem in (
        ("gx", XS, XR, xs_sem, xr_sem), ("gy", YS, YR, ys_sem, yr_sem), ("gz", ZS, ZR, zs_sem, zr_sem)
    ):
        for side, has, target in ((0, here[axis] > 0, -1), (1, here[axis] < counts[axis] - 1, 1)):
            move = pltpu.make_async_remote_copy(
                src_ref=send if axis == "gz" else send.at[side],
                dst_ref=recv.at[1 - side],
                send_sem=send_sem.at[side],
                recv_sem=recv_sem.at[1 - side],
                device_id={axis: here[axis] + target},
                device_id_type=MESH,
            )
            arrival = pltpu.make_async_remote_copy(
                src_ref=send if axis == "gz" else send.at[side],
                dst_ref=recv.at[side],
                send_sem=send_sem.at[side],
                recv_sem=recv_sem.at[side],
                device_id={axis: here[axis] + target},
                device_id_type=MESH,
            )
            moves.append((has, move, arrival, recv, side))

            @pl.when(has)
            def _(move=move):
                move.start()

    @pl.loop(0, cx)
    def _(x_index):
        x = coordinate("gx", cx, jnp.full(tile, x_index, jnp.int32))
        for part in range(cy // 8):
            rows = 8 * part
            y = coordinate("gy", cy, rows + sub)

            def field(comp, dx, dy, rows=rows):
                return F[comp, x_index + 2 + dx, LO + rows + dy : LO + rows + dy + 8, :]

            real, imag = weyl_tile(field, x, y, z)
            PS[0, x_index, rows : rows + 8, :] = real
            PS[1, x_index, rows : rows + 8, :] = imag

    for copy in loads[2:6]:
        copy.wait()
    y_re, y_im, sphere = harmonics(ids_ref[...], theta_ref, phi_ref, table_ref[...])

    for has, move, arrival, recv, side in moves:
        @pl.when(has)
        def _(arrival=arrival):
            arrival.wait_recv()

        @pl.when(jnp.logical_not(has))
        def _(recv=recv, side=side):
            recv[side] = jnp.zeros(recv.shape[1:], jnp.float32)

    for side in range(2):
        for layer in range(2):
            x_at, y_at = layer + side * (cx - 2), layer + side * (cy - 2)
            for c in range(2):
                PS[c, x_at] = PS[c, x_at] + XR[side, c, layer]
                PS[c, :, y_at, :] = PS[c, :, y_at, :] + YR[side, c, layer]
    z_extra = [
        jnp.where(place < 2, pltpu.roll(ZR[1, c], cz - 2, 1), pltpu.roll(ZR[0, c], 2, 1)) for c in range(2)
    ]
    rim = (lane < 2) | (lane >= cz - 2)
    loads[6].wait()
    width = BLK * BLK
    contract = (((1,), (1,)), ((), ()))
    acc = jnp.zeros((2 * cz // BLK, W.shape[0]), jnp.float32)
    for x_index in range(cx):
        pieces = []
        for part in range(cy // 8):
            rows = 8 * part
            both = []
            for c in range(2):
                spot = part * cx + x_index
                extra = pltpu.roll(z_extra[c], cz - 4 * spot, 1) if spot else z_extra[c]
                value = PS[c, x_index, rows : rows + 8, :] + jnp.where(rim, extra, 0.0)
                psi_ref[c, x_index, rows : rows + 8, :] = value.astype(jnp.bfloat16)
                both.append(swap_blocks(value))
            pieces.append(jnp.concatenate(both, 0).astype(jnp.bfloat16))
        acc = acc + lax.dot_general(
            jnp.concatenate(pieces, 1),
            W[:, x_index * width : (x_index + 1) * width],
            contract,
            preferred_element_type=jnp.float32,
        )
    blocks = cz // BLK
    row = lax.broadcasted_iota(jnp.int32, acc.shape, 0)
    slot = lax.broadcasted_iota(jnp.int32, acc.shape, 1)
    acc = jnp.where(row % blocks == slot // PB, acc, 0.0)
    v_re = jnp.sum(acc[:blocks], axis=0, keepdims=True)
    v_im = jnp.sum(acc[blocks:], axis=0, keepdims=True)
    row = lax.broadcasted_iota(jnp.int32, (8, W.shape[0]), 0)
    member = (row >> 1) == sphere
    even = (row & 1) == 0
    v_one = jnp.where(member, jnp.where(even, v_re, v_im), 0.0)
    v_two = jnp.where(member, jnp.where(even, v_im, -v_re), 0.0)
    highest = lax.Precision.HIGHEST
    local = lax.dot_general(v_one, y_re, contract, precision=highest, preferred_element_type=jnp.float32)
    local = local + lax.dot_general(v_two, y_im, contract, precision=highest, preferred_element_type=jnp.float32)
    local = local * (4.0 * math.pi / PTS)
    value = jnp.concatenate([local, jnp.zeros((8, 128 - ROWS), jnp.float32)], 1)

    base = 0
    sends = []
    for phase, (me, count, peer) in enumerate(groups):
        MINE[phase] = value
        copies = [
            pltpu.make_async_remote_copy(
                src_ref=MINE.at[phase],
                dst_ref=RED.at[base + me],
                send_sem=ps_sem.at[base + step],
                recv_sem=pr_sem.at[base + count - step],
                device_id=peer(step),
                device_id_type=MESH,
            )
            for step in range(1, count)
        ]
        for copy in copies:
            copy.start()
        RED[base + me] = value
        for copy in copies:
            copy.wait_recv()
        value = RED[base]
        for other in range(1, count):
            value = value + RED[base + other]
        sends += copies
        base += count
    for s in range(SPHERES):
        modes_ref[s] = value[2 * s : 2 * s + 2, :MODES]
    for copy in sends:
        copy.wait_send()
    for has, move, _, _, _ in moves:
        @pl.when(has)
        def _(move=move):
            move.wait_send()


def shards(counts, metric_pert, curvature, interp_weights, point_ids, theta, phi):
    _, cx, cy, cz = metric_pert.shape
    blocks = interp_weights.shape[2]
    points = theta.shape[0]
    vmem = pl.BlockSpec(memory_space=pltpu.VMEM)
    anywhere = pl.BlockSpec(memory_space=pl.ANY)
    total = counts["gx"] * counts["gy"] + counts["gz"]
    dma = pltpu.SemaphoreType.DMA
    f32 = jnp.float32
    return pl.pallas_call(
        functools.partial(kernel, counts),
        out_shape=(
            pltpu.VMEM((2, cx, cy, cz), jnp.bfloat16),
            pltpu.VMEM((SPHERES, 2, MODES), f32),
        ),
        in_specs=[anywhere] * 7,
        out_specs=(vmem, vmem),
        scratch_shapes=[
            pltpu.VMEM((12, cx + 4, LO + cy + 8, cz), f32),
            pltpu.VMEM((blocks * PB, BLK * BLK * BLK), jnp.bfloat16),
            pltpu.VMEM((blocks, PB), jnp.int32),
            pltpu.VMEM((points // 128, 128), f32),
            pltpu.VMEM((points // 128, 128), f32),
            pltpu.VMEM((ROWS, ROWS), f32),
            pltpu.VMEM((2, cx, cy, cz), f32),
            pltpu.VMEM((2, 2, 2, cy, cz), f32),
            pltpu.VMEM((2, 2, 2, cy, cz), f32),
            pltpu.VMEM((2, 2, 2, cx, cz), f32),
            pltpu.VMEM((2, 2, 2, cx, cz), f32),
            pltpu.VMEM((2, 8, cz), f32),
            pltpu.VMEM((2, 2, 8, cz), f32),
            pltpu.VMEM((total, 8, 128), f32),
            pltpu.VMEM((2, 8, 128), f32),
            dma((7,)), dma((2,)), dma((2,)), dma((2,)), dma((2,)), dma((2,)), dma((2,)),
            dma((total,)), dma((total,)),
        ],
        compiler_params=pltpu.CompilerParams(
            collective_id=0, has_side_effects=True, vmem_limit_bytes=67043328 - 160 * 1024
        ),
    )(
        metric_pert,
        curvature,
        interp_weights.reshape(blocks * PB, BLK * BLK * BLK),
        point_ids.reshape(blocks, PB),
        theta.reshape(points // 128, 128),
        phi.reshape(points // 128, 128),
        jnp.asarray(build_table()),
    )


def solution(mesh):
    in_specs = (
        P(None, "gx", "gy", "gz"),
        P(None, "gx", "gy", "gz"),
        P("gx", "gy", "gz", None, None),
        P("gx", "gy", "gz", None),
        P(),
        P(),
    )
    out_specs = (P(None, "gx", "gy", "gz"), P())
    counts = {axis: mesh.shape[axis] for axis in AXES}
    return jax.shard_map(
        functools.partial(shards, counts), mesh=mesh, in_specs=in_specs, out_specs=out_specs, check_vma=False
    )
```

profile of v0, /device:TPU:0, one launch (start us, length us, event | category | flops | bytes accessed | tf_op | source)
XLA Modules:
  0.0 23.0 jit_solution(8857155521480762834)
XLA Ops:
  0.6 21.1 %shard_map.86 = (bf16[2,16,16,128]{3,2,1,0:T(8,128)(2,1)S(1)}, f32[3,2,77]{2,1,0:T(2,128)S(1)}) custom-call(f32[6,16,16,128]{3,2,1,0:T(8,128)} %metric.1, f32[6,16,16,128]{3,2,1,0:T(8,128)} %curvature.1, bf16[512,4096]{1,0:T(8,128)(2,1)} %bitcast.4, s32[8,64]{1,0:T(8,128)} %bitcast.7, f32[48,128]{1,0:T(8,128)} %bitcast.5, f32[48,128]{1,0:T(8,128)} %bitcast.6, ...), custom_call_target="tpu_custom_call" | custom-call | tf_op jit(solution)/shard_map/pallas_call | solution.py:477
  21.8 0.7 %copy.11 = bf16[2,16,16,128]{3,2,1,0:T(8,128)(2,1)} copy(bf16[2,16,16,128]{3,2,1,0:T(8,128)(2,1)S(1)} %get-tuple-element.2) | data formatting | bytes 262144
  22.4 0.6 %copy.12 = f32[3,2,77]{2,1,0:T(2,128)} copy(f32[3,2,77]{2,1,0:T(2,128)S(1)} %get-tuple-element.3) | data formatting | bytes 3696
where the time goes:
time: 23.1 us; the launch traced here: 23 us
  Pallas kernels  21.1 us (91%)
  local copies, waits for them, and re-layouts  1.24 us (5%)
  between operations  0.64 us (3%)
    pallas_call x1, Pallas kernels, shards(): pl.pallas_call(functools.partial(kernel, counts), out_shape=(pltpu.VMEM((...  21.1 us
    unnamed x2, local copies, waits for them, and re-layouts  1.24 us

commit v1 on v0

v1 whole, which is shorter than its diff:
```python
import functools
import math

import jax
import jax.numpy as jnp
import numpy as np
from jax import lax
from jax.experimental import pallas as pl
from jax.experimental.pallas import tpu as pltpu
from jax.sharding import PartitionSpec as P

BLK = 16
PB = 64
PTS = 2048
SPHERES = 3
LMAX = 8
MODES = (LMAX + 1) ** 2 - 4
ROWS = -(-MODES // 8) * 8
WAVES = -(-(2 * LMAX + 1) // 16) * 16
AXES = ("gx", "gy", "gz")
MESH = pl.DeviceIdType.MESH
LOGICAL = pl.DeviceIdType.LOGICAL
LO = 8
PITCH = 24
DIRECT = 64
HELD = 4


def build_table():
    amplitude = np.zeros((ROWS, WAVES))
    pick_re = np.zeros((ROWS, WAVES))
    pick_im = np.zeros((ROWS, WAVES))
    for degree in range(2, LMAX + 1):
        base = degree * degree - 4
        for order in range(-degree, degree + 1):
            row = base + order + degree
            lead = (-1.0) ** order * math.sqrt(
                math.factorial(degree + order)
                * math.factorial(degree - order)
                * (2 * degree + 1)
                / (4.0 * math.pi * math.factorial(degree - 2) * math.factorial(degree + 2))
            )
            for step in range(0, degree + 3):
                lower = step - 2 - order
                if 0 <= lower <= degree - 2:
                    scale = (
                        lead
                        * math.comb(degree + 2, step)
                        * math.comb(degree - 2, lower)
                        * (-1.0) ** (degree - step + 2)
                    )
                    up, down = 2 * step - 2 - order, 2 * degree - 2 * step + 2 + order
                    wave = [1.0 + 0.0j]
                    for one, two in [(0.5, 0.5)] * up + [(-0.5j, 0.5j)] * down:
                        longer = [0.0j] * (len(wave) + 1)
                        for place, value in enumerate(wave):
                            longer[place + 1] += value * one
                            longer[place] += value * two
                        wave = longer
                    for j in range(degree + 1):
                        high, low = wave[degree + j], wave[degree - j]
                        amplitude[row, j] += scale * ((high + low).real if j else high.real)
                        if j:
                            amplitude[row, LMAX + j] += scale * (1j * (high - low)).real
            size = abs(order)
            pick_re[row, size] = 1.0
            if size:
                pick_im[row, LMAX + size] = 1.0 if order > 0 else -1.0
    table = np.concatenate([amplitude, pick_re, pick_im], 0).astype(np.float32)
    pieces = []
    for _ in range(3):
        pieces.append(table.astype(jnp.bfloat16))
        table = table - pieces[-1].astype(np.float32)
    return np.concatenate([pieces[n] for n in (0, 0, 1, 0, 1, 2)], 1)


def split(value, count):
    pieces = []
    for _ in range(count - 1):
        pieces.append(value.astype(jnp.bfloat16))
        value = value - pieces[-1].astype(jnp.float32)
    return pieces + [value.astype(jnp.bfloat16)]


def waves(gz, spacing, ids, theta_ref, phi_ref, wave_ref):
    blocks, slots = ids.shape
    per = PTS // 128
    wide = jnp.concatenate([ids] * (128 // slots), 1)
    low = lax.div(gz * blocks, spacing)
    high = jnp.minimum(low + 1, SPHERES - 1)
    layer = gz * blocks + lax.broadcasted_iota(jnp.int32, wide.shape, 0)
    later = layer >= (low + 1) * spacing
    point = wide - jnp.where(later, low + 1, low) * PTS
    row, lane = point >> 7, point & 127
    first = lax.broadcasted_iota(jnp.int32, wide.shape, 1) < slots
    angle = jnp.zeros(wide.shape, jnp.float32)

    def look_up(ref, index):
        one = jnp.broadcast_to(ref[pl.ds(low * per + index, 1), :], wide.shape)
        two = jnp.broadcast_to(ref[pl.ds(high * per + index, 1), :], wide.shape)
        return jnp.take_along_axis(jnp.where(later, two, one), lane, axis=1)

    for index in range(per):
        found = jnp.where(first, look_up(theta_ref, index), look_up(phi_ref, index))
        angle = jnp.where(row == index, found, angle)
    re, im = [jnp.ones(wide.shape, jnp.float32), jnp.cos(angle)], [None, jnp.sin(angle)]
    for j in range(2, LMAX + 1):
        a, b = j // 2, j - j // 2
        re.append(re[a] * re[b] - im[a] * im[b])
        im.append(re[a] * im[b] + im[a] * re[b])
    rows = re + im[1:]
    rows += [jnp.zeros(wide.shape, jnp.float32)] * (WAVES - len(rows))
    for place, value in enumerate(rows):
        wave_ref[place * blocks : (place + 1) * blocks, :] = value
    lane = lax.broadcasted_iota(jnp.int32, (8, 128), 1)
    result = [[], []]
    for pair in range(0, blocks, 2):
        columns = [[], []]
        for group in range(WAVES // 8):
            one = wave_ref[pl.ds(group * 8 * blocks + pair, 8, blocks), :]
            two = wave_ref[pl.ds(group * 8 * blocks + pair + 1, 8, blocks), :]
            columns[0].append(jnp.where(lane < slots, one, pltpu.roll(two, slots, 1)))
            columns[1].append(jnp.where(lane < slots, pltpu.roll(one, slots, 1), two))
        for side in range(2):
            result[side].append(jnp.concatenate(columns[side], 0))
    return tuple(jnp.concatenate(parts, 1) for parts in result)


def harmonics(in_theta, in_phi, table):
    def expand(rows, value):
        one, two, three = split(value, 3)
        stack = jnp.concatenate([one, two, one, three, two, one], 0)
        return jnp.dot(rows, stack, preferred_element_type=jnp.float32)

    amplitude = expand(table[:ROWS], in_theta)
    picked = expand(table[ROWS:], in_phi)
    re, im = split(amplitude * picked[:ROWS], 2), split(amplitude * picked[ROWS:], 2)
    return [jnp.concatenate([re[n], im[n]], 1) for n in range(2)]


def frame(x, y, z):
    rho2 = x * x + y * y
    inv_rho = lax.rsqrt(rho2)
    inv_radius = lax.rsqrt(rho2 + z * z)
    c, s = x * inv_rho, y * inv_rho
    cos_theta, sin_theta = z * inv_radius, rho2 * inv_rho * inv_radius
    cc, ss, cs = c * c, s * s, c * s
    square = cos_theta * cos_theta
    down = sin_theta * (1.0 / 24.0)
    cross = cos_theta * down
    turn = cos_theta * (1.0 / 24.0)
    return (
        (square * ss - cc) * (0.5 / 24.0), sin_theta * sin_theta * (0.5 / 24.0),
        (square + 1.0) * cs * (1.0 / 24.0), -cross * c, -cross * s,
        turn * cs, turn * (cc - ss), s * down, -c * down,
    )


def contract(weights, electric, magnetic):
    p, q = weights[:5], (weights[5], None) + tuple(weights[6:])

    def dot(weight, values):
        total = None
        for one, two in zip(weight, values):
            if one is not None and two is not None:
                total = one * two if total is None else total + one * two
        return total

    return -dot(p, electric) - dot(q, magnetic), dot(q, electric) - dot(p, magnetic)


def twist(a, b, c):
    one, two = b - a, b - c
    both = one + two
    return both + both, (one + one - two) * 2.0


def face_tile(axis, weights, laplace, deriv):
    electric = [laplace(comp) for comp in (3, 5, 1, 2, 4)]
    if axis == 0:
        c = deriv(10) * 2.0
        magnetic = (-c, c, -deriv(8), deriv(7), deriv(0))
    elif axis == 1:
        a = deriv(8) * -2.0
        magnetic = (a, a + a, deriv(10), deriv(11), -deriv(7))
    else:
        b = deriv(7) * 2.0
        magnetic = (b + b, b, -deriv(9), -deriv(10), deriv(8))
    return contract(weights, electric, magnetic)


def weyl_tile(field, weights):
    def along(comp, axis, offset):
        if axis == 0:
            return field(comp, offset, 0)
        if axis == 1:
            return field(comp, 0, offset)
        value = field(comp, 0, 0)
        return pltpu.roll(value, (-offset) % value.shape[1], 1)

    def first(comp, axis):
        near = along(comp, axis, 1) - along(comp, axis, -1)
        return near * 8.0 - (along(comp, axis, 2) - along(comp, axis, -2))

    xx, xy, xz, yy, yz, over = [field(6 + comp, 0, 0) for comp in range(6)]
    zz = over + xx
    part = yy - xx
    last = part.shape[1]
    yz2 = yz * yz
    square = (
        yz2 - xz * xz - part * zz,
        yz2 - xy * xy - yy * over,
        xz * yz - xy * zz,
        xy * yz - xz * yy,
        xy * xz - xx * yz,
    )
    electric = []
    for comp, value in zip((3, 5, 1, 2, 4), square):
        near, far = None, None
        for axis in range(3):
            one = along(comp, axis, 1) + along(comp, axis, -1)
            two = along(comp, axis, 2) + along(comp, axis, -2)
            near, far = (one, two) if near is None else (near + one, far + two)
        electric.append(value * 24.0 + near * 16.0 - far - field(comp, 0, 0) * 90.0)
    part_z = (pltpu.roll(part, last - 1, 1) - pltpu.roll(part, 1, 1)) * 8.0 - (
        pltpu.roll(part, last - 2, 1) - pltpu.roll(part, 2, 1)
    )
    magnetic = twist(first(8, 1), first(7, 2), first(10, 0)) + (
        first(10, 1) - part_z - first(8, 0),
        first(11, 1) - first(10, 2) + first(7, 0),
        first(8, 2) + first(0, 0) - first(7, 1),
    )
    return contract(weights, electric, magnetic)


def swap_blocks(tile):
    count = tile.shape[0]
    width = tile.shape[1] // count
    rolled = pltpu.roll(tile, 0, 1, stride=width, stride_axis=0)
    row = lax.broadcasted_iota(jnp.int32, tile.shape, 0)
    block = lax.broadcasted_iota(jnp.int32, tile.shape, 1) // width
    mixed = jnp.take_along_axis(rolled, (block - row + count) % count, axis=0)
    out = mixed
    for bit in range(3):
        shift = (1 << bit) * width
        out = jnp.where((row >> bit) & 1 == 1, pltpu.roll(out, tile.shape[1] - shift, 1), out)
    return out


def kernel(
    counts, metric, curvature, weights, ids_hbm, theta_hbm, phi_hbm, table_hbm,
    psi_ref, modes_ref,
    F, W, ids_ref, theta_ref, phi_ref, table_ref, wave_ref, FRAME, EDGE, POLL, T,
    PS, XS, XR, YS, YR, ZS, ZR, RED, MINE,
    load_sem, xs_sem, xr_sem, ys_sem, yr_sem, zs_sem, zr_sem, ps_sem, pr_sem,
):
    cx, cy, cz = psi_ref.shape[1:]
    blocks = cz // BLK
    spacing = blocks * counts["gz"] // SPHERES
    here = {axis: lax.axis_index(axis) for axis in AXES}
    loads = [
        pltpu.make_async_copy(source, target, load_sem.at[place])
        for place, (source, target) in enumerate((
            (metric, F.at[pl.ds(0, 6), pl.ds(2, cx), pl.ds(LO, cy)]),
            (curvature, F.at[pl.ds(6, 6), pl.ds(2, cx), pl.ds(LO, cy)]),
            (ids_hbm, ids_ref),
            (theta_hbm, theta_ref),
            (phi_hbm, phi_ref),
            (table_hbm, table_ref),
            (weights, W),
        ))
    ]
    for copy in loads:
        copy.start()

    def group_of(axes):
        total, rank, own = 1, 0, 0
        stride = math.prod(counts.values())
        strides = {}
        for axis in AXES:
            stride //= counts[axis]
            strides[axis] = stride
            own = own + here[axis] * stride
        for axis in axes:
            total *= counts[axis]
            rank = rank * counts[axis] + here[axis]
        unit = strides[axes[-1]]

        def peer(step):
            other = lax.rem(rank + step, total)
            return own + (other - rank) * unit

        return rank, total, peer

    if math.prod(counts.values()) <= DIRECT:
        groups = (group_of(AXES),)
    else:
        groups = (group_of(("gx", "gy")), group_of(("gz",)))
    barrier = pltpu.get_barrier_semaphore()
    with jax.named_scope("signal"):
        for _, count, peer in groups:
            for step in range(1, count):
                pl.semaphore_signal(barrier, inc=1, device_id=peer(step), device_id_type=LOGICAL)

    def coordinate(axis, cells, index):
        return (here[axis] * cells + index).astype(jnp.float32) + (0.5 - counts[axis] * cells / 2.0)

    tile = (8, cz)
    sub = lax.broadcasted_iota(jnp.int32, tile, 0)
    lane = lax.broadcasted_iota(jnp.int32, tile, 1)
    z = coordinate("gz", cz, lane)
    spot_of = ((lane + 2) & (cz - 1)) >> 2
    place = (lane + 2) & 3

    def layers(cells):
        return (
            (0, 0, -2, None, 0), (0, 1, -1, 0, 1),
            (1, 0, cells, cells - 1, cells - 2), (1, 1, cells + 1, None, cells - 1),
        )

    with jax.named_scope("zero"):
        for edge in (0, cx + 2):
            F[:, edge : edge + 2, LO : LO + cy, :] = jnp.zeros((12, 2, cy, cz), jnp.float32)
        for edge in (LO - 8, LO + cy):
            F[:, 2 : 2 + cx, edge : edge + 8, :] = jnp.zeros((12, cx, 8, cz), jnp.float32)
    with jax.named_scope("frames"):
        @pl.loop(0, cx)
        def _(x_index):
            x = coordinate("gx", cx, jnp.full(tile, x_index, jnp.int32))
            for part in range(cy // 8):
                for n, value in enumerate(frame(x, coordinate("gy", cy, sub + 8 * part), z)):
                    FRAME[n, x_index, 8 * part : 8 * part + 8, :] = value

        for at, (side, layer, cell, _, _) in enumerate(layers(cx)):
            for part in range(cy // 8):
                x = coordinate("gx", cx, jnp.full(tile, cell, jnp.int32))
                for n, value in enumerate(frame(x, coordinate("gy", cy, sub + 8 * part), z)):
                    EDGE[n, at, 8 * part : 8 * part + 8, :] = value
        for at, (side, layer, cell, _, _) in enumerate(layers(cy)):
            for part in range(cx // 8):
                y = coordinate("gy", cy, jnp.full(tile, cell, jnp.int32))
                for n, value in enumerate(frame(coordinate("gx", cx, sub + 8 * part), y, z)):
                    EDGE[n, 4 + at, 8 * part : 8 * part + 8, :] = value
        x = coordinate("gx", cx, spot_of % cx)
        y = coordinate("gy", cy, (spot_of // cx) * 8 + sub)
        beyond = coordinate("gz", cz, jnp.where(place >= 2, place - 4, cz + place))
        within = coordinate("gz", cz, jnp.where(place >= 2, cz + place - 4, place))
        for n, value in enumerate(frame(x, y, beyond)):
            EDGE[n, 8, :8, :] = value
        for n, value in enumerate(frame(x, y, within)):
            EDGE[n, 8, 8:16, :] = value

    with jax.named_scope("wait_fields"):
        loads[0].wait()
        loads[1].wait()

    with jax.named_scope("prepare"):
        @pl.loop(0, cx)
        def _(x_index):
            for part in range(cy // 8):
                rows = slice(LO + 8 * part, LO + 8 * part + 8)
                at = 2 + x_index
                h_xx, k_xx, k_zz = F[0, at, rows, :], F[6, at, rows, :], F[11, at, rows, :]
                F[3, at, rows, :] = F[3, at, rows, :] - h_xx
                F[5, at, rows, :] = F[5, at, rows, :] - h_xx
                F[0, at, rows, :] = F[9, at, rows, :] - k_zz
                F[11, at, rows, :] = k_zz - k_xx

    def face(axis, at, part, sign, near, far):
        def laplace(comp):
            return -far(comp) if near is None else near(comp) * 16.0 - far(comp)

        def deriv(comp):
            value = -far(comp) if near is None else near(comp) * 8.0 - far(comp)
            return value * sign

        weight = tuple(EDGE[n, at, 8 * part : 8 * part + 8, :] for n in range(9))
        return face_tile(axis, weight, laplace, functools.lru_cache(None)(deriv))

    with jax.named_scope("faces_x"):
        for at, (side, layer, _, near, far) in enumerate(layers(cx)):
            for part in range(cy // 8):
                rows = slice(LO + 8 * part, LO + 8 * part + 8)
                load = lambda at, rows=rows: None if at is None else lambda comp: F[comp, 2 + at, rows, :]
                real, imag = face(0, at, part, 1.0 - 2.0 * side, load(near), load(far))
                XS[side, 0, layer, 8 * part : 8 * part + 8, :] = real
                XS[side, 1, layer, 8 * part : 8 * part + 8, :] = imag
    pitch = F.shape[2]
    flat = F.reshape(12 * F.shape[1] * pitch, cz)
    with jax.named_scope("faces_y"):
        for at, (side, layer, _, near, far) in enumerate(layers(cy)):
            for part in range(cx // 8):
                start = (2 + 8 * part) * pitch + LO
                load = lambda at, start=start: None if at is None else lambda comp: flat[
                    pl.ds(comp * F.shape[1] * pitch + start + at, 8, pitch), :
                ]
                real, imag = face(1, 4 + at, part, 1.0 - 2.0 * side, load(near), load(far))
                YS[side, 0, layer, 8 * part : 8 * part + 8, :] = real
                YS[side, 1, layer, 8 * part : 8 * part + 8, :] = imag

    with jax.named_scope("faces_z"):
        @functools.lru_cache(None)
        def z_edges(comp):
            packed = None
            for part in range(cy // 8):
                rows = slice(LO + 8 * part, LO + 8 * part + 8)
                for x in range(cx):
                    spot = part * cx + x
                    moved = F[comp, 2 + x, rows, :]
                    if comp == 9:
                        moved = moved - F[6, 2 + x, rows, :]
                    if spot:
                        moved = jnp.where(spot_of == spot, pltpu.roll(moved, 4 * spot, 1), packed)
                    packed = moved
            return packed

        @functools.lru_cache(None)
        def z_near(comp):
            edges = z_edges(comp)
            return jnp.where(
                place == 3, pltpu.roll(edges, 1, 1), jnp.where(place == 0, pltpu.roll(edges, cz - 1, 1), 0.0)
            )

        sign = jnp.where(place >= 2, 1.0, -1.0)
        real, imag = face(2, 8, 0, sign, z_near, z_edges)
        ZS[0] = real
        ZS[1] = imag
        real, imag = face(2, 8, 1, sign, z_near, z_edges)
        POLL[0] = real
        POLL[1] = imag

    with jax.named_scope("barrier"):
        pl.semaphore_wait(barrier, sum(count - 1 for _, count, _ in groups))

    moves = []
    for axis, send, recv, send_sem, recv_sem in (
        ("gx", XS, XR, xs_sem, xr_sem), ("gy", YS, YR, ys_sem, yr_sem), ("gz", ZS, ZR, zs_sem, zr_sem)
    ):
        for side, has, target in ((0, here[axis] > 0, -1), (1, here[axis] < counts[axis] - 1, 1)):
            move = pltpu.make_async_remote_copy(
                src_ref=send if axis == "gz" else send.at[side],
                dst_ref=recv.at[1 - side],
                send_sem=send_sem.at[side],
                recv_sem=recv_sem.at[1 - side],
                device_id={axis: here[axis] + target},
                device_id_type=MESH,
            )
            arrival = pltpu.make_async_remote_copy(
                src_ref=send if axis == "gz" else send.at[side],
                dst_ref=recv.at[side],
                send_sem=send_sem.at[side],
                recv_sem=recv_sem.at[side],
                device_id={axis: here[axis] + target},
                device_id_type=MESH,
            )
            moves.append((has, move, arrival, recv, side))

            @pl.when(has)
            def _(move=move):
                move.start()

    with jax.named_scope("stencil"):
        @pl.loop(0, cx, unroll=16)
        def _(x_index):
            for part in range(cy // 8):
                rows = 8 * part

                def field(comp, dx, dy, rows=rows):
                    return F[comp, x_index + 2 + dx, LO + rows + dy : LO + rows + dy + 8, :]

                weight = tuple(FRAME[n, x_index, rows : rows + 8, :] for n in range(9))
                real, imag = weyl_tile(field, weight)
                PS[0, x_index, rows : rows + 8, :] = real
                PS[1, x_index, rows : rows + 8, :] = imag

    with jax.named_scope("harmonics"):
        for copy in loads[2:6]:
            copy.wait()
        ids = ids_ref[...]
        y_high, y_low = harmonics(*waves(here["gz"], spacing, ids, theta_ref, phi_ref, wave_ref), table_ref[...])
        sphere = jnp.concatenate([ids[b : b + 1] for b in range(ids.shape[0])], 1) // PTS

    with jax.named_scope("wait_halo"):
        for has, move, arrival, recv, side in moves:
            @pl.when(has)
            def _(arrival=arrival):
                arrival.wait_recv()

            @pl.when(jnp.logical_not(has))
            def _(recv=recv, side=side):
                recv[side] = jnp.zeros(recv.shape[1:], jnp.float32)

    with jax.named_scope("add_faces"):
        for side in range(2):
            for layer in range(2):
                x_at, y_at = layer + side * (cx - 2), layer + side * (cy - 2)
                for c in range(2):
                    PS[c, x_at] = PS[c, x_at] + XR[side, c, layer]
                    PS[c, :, y_at, :] = PS[c, :, y_at, :] + YR[side, c, layer]
        z_extra = [
            jnp.where(
                place < 2, pltpu.roll(ZR[1, c] - POLL[c], cz - 2, 1), pltpu.roll(ZR[0, c] - POLL[c], 2, 1)
            )
            for c in range(2)
        ]
    with jax.named_scope("wait_w"):
        loads[6].wait()
    with jax.named_scope("swap"):
        rim = (lane < 2) | (lane >= cz - 2)
        width = BLK * BLK
        for x_index in range(cx):
            parts = [[], []]
            for part in range(cy // 8):
                rows = 8 * part
                for c in range(2):
                    spot = part * cx + x_index
                    extra = pltpu.roll(z_extra[c], cz - 4 * spot, 1) if spot else z_extra[c]
                    parts[c].append(PS[c, x_index, rows : rows + 8, :] + jnp.where(rim, extra, 0.0))
            for c in range(2):
                psi_ref[c, x_index] = jnp.concatenate(parts[c], 0).astype(jnp.bfloat16)
            for part in range(cy // 8):
                both = [swap_blocks(parts[c][part]) for c in range(2)]
                at = x_index * width + part * 8 * BLK
                T[:, at : at + 8 * BLK] = jnp.concatenate(both, 0).astype(jnp.bfloat16)
    across = (((1,), (1,)), ((), ()))
    with jax.named_scope("interp"):
        acc = lax.dot_general(T[...], W[...], across, preferred_element_type=jnp.float32)
    with jax.named_scope("project"):
        row = lax.broadcasted_iota(jnp.int32, acc.shape, 0)
        slot = lax.broadcasted_iota(jnp.int32, acc.shape, 1)
        acc = jnp.where(row % blocks == slot // PB, acc, 0.0)
        v_re = jnp.sum(acc[:blocks], axis=0, keepdims=True)
        v_im = jnp.sum(acc[blocks:], axis=0, keepdims=True)
        row = lax.broadcasted_iota(jnp.int32, (8, W.shape[0]), 0)
        member = (row >> 1) + lax.div(here["gz"] * blocks, spacing) == sphere
        even = (row & 1) == 0
        v_one = jnp.where(member, jnp.where(even, v_re, v_im), 0.0)
        v_two = jnp.where(member, jnp.where(even, v_im, -v_re), 0.0)
        both = jnp.concatenate([v_one, v_two], 1) * (4.0 * math.pi / PTS)
        rest = both - both.astype(jnp.bfloat16).astype(jnp.float32)
        both = jnp.concatenate([both, rest], 0).astype(jnp.bfloat16)
        one = lax.dot_general(both, y_high, across, preferred_element_type=jnp.float32)
        two = lax.dot_general(both, y_low, across, preferred_element_type=jnp.float32)
        local = one[:8] + one[8:] + (two[:8] + two[8:])
        value = jnp.concatenate([local[:HELD], jnp.zeros((HELD, 128 - ROWS), jnp.float32)], 1)

    base = 0
    sends = []
    for phase, (me, count, peer) in enumerate(groups):
        with jax.named_scope(f"reduce{phase}"):
            MINE[phase] = value
            copies = [
                pltpu.make_async_remote_copy(
                    src_ref=MINE.at[phase],
                    dst_ref=RED.at[base + me],
                    send_sem=ps_sem.at[phase],
                    recv_sem=pr_sem.at[phase],
                    device_id=peer(step),
                    device_id_type=LOGICAL,
                )
                for step in range(1, count)
            ]
            for copy in copies:
                copy.start()
            RED[base + me] = value
        everything = pltpu.make_async_remote_copy(
            src_ref=RED.at[pl.ds(base, count - 1)],
            dst_ref=RED.at[pl.ds(base, count - 1)],
            send_sem=ps_sem.at[phase],
            recv_sem=pr_sem.at[phase],
            device_id=peer(1),
            device_id_type=LOGICAL,
        )
        with jax.named_scope(f"gather{phase}"):
            everything.wait_recv()
            last = phase == len(groups) - 1
            sums = []
            for lot in range(counts["gz"] if last else 1):
                members = range(lot, count, counts["gz"]) if last else range(count)
                value = None
                for other in members:
                    value = RED[base + other] if value is None else value + RED[base + other]
                sums.append(value)
        sends.append(everything)
        base += count
    for s in range(SPHERES):
        total = None
        for lot in range(counts["gz"]):
            at = 2 * (s - lot * blocks // spacing)
            if 0 <= at < HELD:
                piece = sums[lot][at : at + 2, :MODES]
                total = piece if total is None else total + piece
        modes_ref[s] = total
    with jax.named_scope("tail"):
        for copy in sends:
            copy.wait_send()
        for has, move, _, _, _ in moves:
            @pl.when(has)
            def _(move=move):
                move.wait_send()


def store_kernel(psi_ref, modes_ref, psi_out, modes_out, sem):
    copies = [
        pltpu.make_async_copy(psi_ref, psi_out, sem.at[0]),
        pltpu.make_async_copy(modes_ref, modes_out, sem.at[1]),
    ]
    for copy in copies:
        copy.start()
    for copy in copies:
        copy.wait()


def shards(counts, metric_pert, curvature, interp_weights, point_ids, theta, phi):
    _, cx, cy, cz = metric_pert.shape
    blocks = interp_weights.shape[2]
    points = theta.shape[0]
    vmem = pl.BlockSpec(memory_space=pltpu.VMEM)
    anywhere = pl.BlockSpec(memory_space=pl.ANY)
    many = math.prod(counts.values())
    total = many if many <= DIRECT else counts["gx"] * counts["gy"] + counts["gz"]
    phases = 1 if many <= DIRECT else 2
    dma = pltpu.SemaphoreType.DMA
    f32 = jnp.float32
    table = build_table()
    psi, modes = pl.pallas_call(
        functools.partial(kernel, counts),
        out_shape=(
            pltpu.VMEM((2, cx, cy, cz), jnp.bfloat16),
            pltpu.VMEM((SPHERES, 2, MODES), f32),
        ),
        in_specs=[anywhere] * 7,
        out_specs=(vmem, vmem),
        scratch_shapes=[
            pltpu.VMEM((12, cx + 5, LO + cy + PITCH - 8, cz), f32),
            pltpu.VMEM((blocks * PB, BLK * BLK * BLK), jnp.bfloat16),
            pltpu.VMEM((blocks, PB), jnp.int32),
            pltpu.VMEM((points // 128, 128), f32),
            pltpu.VMEM((points // 128, 128), f32),
            pltpu.VMEM(table.shape, jnp.bfloat16),
            pltpu.VMEM((WAVES * blocks, 128), f32),
            pltpu.VMEM((9, cx, cy, cz), f32),
            pltpu.VMEM((9, 9, 16, cz), f32),
            pltpu.VMEM((2, 8, cz), f32),
            pltpu.VMEM((2 * blocks, BLK * BLK * BLK), jnp.bfloat16),
            pltpu.VMEM((2, cx, cy, cz), f32),
            pltpu.VMEM((2, 2, 2, cy, cz), f32),
            pltpu.VMEM((2, 2, 2, cy, cz), f32),
            pltpu.VMEM((2, 2, 2, cx, cz), f32),
            pltpu.VMEM((2, 2, 2, cx, cz), f32),
            pltpu.VMEM((2, 8, cz), f32),
            pltpu.VMEM((2, 2, 8, cz), f32),
            pltpu.VMEM((total, HELD, 128), f32),
            pltpu.VMEM((2, HELD, 128), f32),
            dma((7,)), dma((2,)), dma((2,)), dma((2,)), dma((2,)), dma((2,)), dma((2,)),
            dma((phases,)), dma((phases,)),
        ],
        compiler_params=pltpu.CompilerParams(
            collective_id=0, has_side_effects=True, vmem_limit_bytes=60 * 1024 * 1024
        ),
    )(
        metric_pert,
        curvature,
        interp_weights.reshape(blocks * PB, BLK * BLK * BLK),
        point_ids.reshape(blocks, PB),
        theta.reshape(points // 128, 128),
        phi.reshape(points // 128, 128),
        jnp.asarray(table),
    )
    return pl.pallas_call(
        store_kernel,
        out_shape=(
            jax.ShapeDtypeStruct(psi.shape, psi.dtype),
            jax.ShapeDtypeStruct(modes.shape, modes.dtype),
        ),
        in_specs=[vmem, vmem],
        out_specs=(anywhere, anywhere),
        scratch_shapes=[dma((2,))],
        compiler_params=pltpu.CompilerParams(vmem_limit_bytes=1024 * 1024),
    )(psi, modes)


def solution(mesh):
    in_specs = (
        P(None, "gx", "gy", "gz"),
        P(None, "gx", "gy", "gz"),
        P("gx", "gy", "gz", None, None),
        P("gx", "gy", "gz", None),
        P(),
        P(),
    )
    out_specs = (P(None, "gx", "gy", "gz"), P())
    counts = {axis: mesh.shape[axis] for axis in AXES}
    return jax.shard_map(
        functools.partial(shards, counts), mesh=mesh, in_specs=in_specs, out_specs=out_specs, check_vma=False
    )
```

time: 23.1 us -> 17.7 us (0.77)
  Pallas kernels: 21.1 us -> 16.9 us
  local copies, waits for them, and re-layouts: 1.24 us -> 0 us
    pallas_call x1, Pallas kernels: 21.1 us -> 16.2 us  [shards(): pl.pallas_call(functools.partial(kernel, counts), out_shape=(pltpu.VMEM((...]
    unnamed x2 -> x0, local copies, waits for them, and re-layouts: 1.24 us -> none
    pallas_call x0 -> x1, Pallas kernels: none -> 0.68 us  [shards(): pl.pallas_call(store_kernel, out_shape=(jax.ShapeDtypeStruct(psi.shape, p...]
where the time goes in v1:
time: 17.7 us; the launch traced here: 17.5 us
  Pallas kernels  16.9 us (95%)
  between operations  0.64 us (4%)
    pallas_call x1, Pallas kernels, shards(): pl.pallas_call(functools.partial(kernel, counts), out_shape=(pltpu.VMEM((...  16.2 us
    pallas_call x1, Pallas kernels, shards(): pl.pallas_call(store_kernel, out_shape=(jax.ShapeDtypeStruct(psi.shape, p...  0.68 us

profile of v1, /device:TPU:0, one launch (start us, length us, event | category | flops | bytes accessed | tf_op | source)
XLA Modules:
  0.0 17.5 jit_solution(6071345714781136061)
XLA Ops:
  0.6 16.2 %shard_map.86 = (bf16[2,16,16,128]{3,2,1,0:T(8,128)(2,1)S(1)}, f32[3,2,77]{2,1,0:T(2,128)S(1)}) custom-call(f32[6,16,16,128]{3,2,1,0:T(8,128)} %metric.1, f32[6,16,16,128]{3,2,1,0:T(8,128)} %curvature.1, bf16[512,4096]{1,0:T(8,128)(2,1)} %bitcast.4, s32[8,64]{1,0:T(8,128)} %bitcast.7, f32[48,128]{1,0:T(8,128)} %bitcast.5, f32[48,128]{1,0:T(8,128)} %bitcast.6, ...), custom_call_target="tpu_custom_call" | custom-call | tf_op jit(solution)/shard_map/pallas_call | solution.py:626
  16.9 0.7 %shard_map.87 = (bf16[2,16,16,128]{3,2,1,0:T(8,128)(2,1)}, f32[3,2,77]{2,1,0:T(2,128)}) custom-call(bf16[2,16,16,128]{3,2,1,0:T(8,128)(2,1)S(1)} %get-tuple-element.4.psi_ref, f32[3,2,77]{2,1,0:T(2,128)S(1)} %get-tuple-element.5.modes_ref), custom_call_target="tpu_custom_call" | custom-call | tf_op jit(solution)/shard_map/pallas_call | solution.py:670

commit v2 on v1

--- a/solution.py
+++ b/solution.py
@@ -239,12 +239,8 @@
     rolled = pltpu.roll(tile, 0, 1, stride=width, stride_axis=0)
     row = lax.broadcasted_iota(jnp.int32, tile.shape, 0)
     block = lax.broadcasted_iota(jnp.int32, tile.shape, 1) // width
-    mixed = jnp.take_along_axis(rolled, (block - row + count) % count, axis=0)
-    out = mixed
-    for bit in range(3):
-        shift = (1 << bit) * width
-        out = jnp.where((row >> bit) & 1 == 1, pltpu.roll(out, tile.shape[1] - shift, 1), out)
-    return out
+    mixed = jnp.take_along_axis(rolled, (block + row + 1) % count, axis=0)
+    return pltpu.roll(mixed, width, 1, stride=width, stride_axis=0)
 
 
 def kernel(
@@ -270,8 +266,8 @@
             (weights, W),
         ))
     ]
-    for copy in loads:
-        copy.start()
+    for at in (2, 3, 4, 5, 0, 1):
+        loads[at].start()
 
     def group_of(axes):
         total, rank, own = 1, 0, 0
@@ -286,11 +282,17 @@
             rank = rank * counts[axis] + here[axis]
         unit = strides[axes[-1]]
 
+        def target(other):
+            return other if len(axes) == len(AXES) else own + (other - rank) * unit
+
         def peer(step):
-            other = lax.rem(rank + step, total)
-            return own + (other - rank) * unit
-
-        return rank, total, peer
+            other = (rank + step) & (total - 1) if total & (total - 1) == 0 else lax.rem(rank + step, total)
+            return target(other)
+
+        def rising(step):
+            return target(jnp.where(rank <= step - 1, step, step - 1))
+
+        return rank, total, peer, rising
 
     if math.prod(counts.values()) <= DIRECT:
         groups = (group_of(AXES),)
@@ -298,8 +300,10 @@
         groups = (group_of(("gx", "gy")), group_of(("gz",)))
     barrier = pltpu.get_barrier_semaphore()
     with jax.named_scope("signal"):
-        for _, count, peer in groups:
-            for step in range(1, count):
+        strides = [1, counts["gz"], counts["gy"] * counts["gz"]]
+        for _, count, peer, _ in groups:
+            near = [step for step in range(1, count) if min(step, count - step) in strides]
+            for step in near + [step for step in range(1, count) if step not in near]:
                 pl.semaphore_signal(barrier, inc=1, device_id=peer(step), device_id_type=LOGICAL)
 
     def coordinate(axis, cells, index):
@@ -319,12 +323,13 @@
         )
 
     with jax.named_scope("zero"):
-        for edge in (0, cx + 2):
-            F[:, edge : edge + 2, LO : LO + cy, :] = jnp.zeros((12, 2, cy, cz), jnp.float32)
-        for edge in (LO - 8, LO + cy):
-            F[:, 2 : 2 + cx, edge : edge + 8, :] = jnp.zeros((12, cx, 8, cz), jnp.float32)
+        for first, last in ((0, 6), (7, 9), (10, 12)):
+            for edge in (0, cx + 2):
+                F[first:last, edge : edge + 2, LO : LO + cy, :] = jnp.zeros((last - first, 2, cy, cz), jnp.float32)
+            for edge in (LO - 8, LO + cy):
+                F[first:last, 2 : 2 + cx, edge : edge + 8, :] = jnp.zeros((last - first, cx, 8, cz), jnp.float32)
     with jax.named_scope("frames"):
-        @pl.loop(0, cx)
+        @pl.loop(0, cx, unroll=4)
         def _(x_index):
             x = coordinate("gx", cx, jnp.full(tile, x_index, jnp.int32))
             for part in range(cy // 8):
@@ -350,9 +355,17 @@
         for n, value in enumerate(frame(x, y, within)):
             EDGE[n, 8, 8:16, :] = value
 
+    with jax.named_scope("harmonics"):
+        for copy in loads[2:6]:
+            copy.wait()
+        ids = ids_ref[...]
+        y_high, y_low = harmonics(*waves(here["gz"], spacing, ids, theta_ref, phi_ref, wave_ref), table_ref[...])
+        sphere = jnp.concatenate([ids[b : b + 1] for b in range(ids.shape[0])], 1) // PTS
+
     with jax.named_scope("wait_fields"):
         loads[0].wait()
         loads[1].wait()
+        loads[6].start()
 
     with jax.named_scope("prepare"):
         @pl.loop(0, cx)
@@ -377,65 +390,9 @@
         weight = tuple(EDGE[n, at, 8 * part : 8 * part + 8, :] for n in range(9))
         return face_tile(axis, weight, laplace, functools.lru_cache(None)(deriv))
 
-    with jax.named_scope("faces_x"):
-        for at, (side, layer, _, near, far) in enumerate(layers(cx)):
-            for part in range(cy // 8):
-                rows = slice(LO + 8 * part, LO + 8 * part + 8)
-                load = lambda at, rows=rows: None if at is None else lambda comp: F[comp, 2 + at, rows, :]
-                real, imag = face(0, at, part, 1.0 - 2.0 * side, load(near), load(far))
-                XS[side, 0, layer, 8 * part : 8 * part + 8, :] = real
-                XS[side, 1, layer, 8 * part : 8 * part + 8, :] = imag
-    pitch = F.shape[2]
-    flat = F.reshape(12 * F.shape[1] * pitch, cz)
-    with jax.named_scope("faces_y"):
-        for at, (side, layer, _, near, far) in enumerate(layers(cy)):
-            for part in range(cx // 8):
-                start = (2 + 8 * part) * pitch + LO
-                load = lambda at, start=start: None if at is None else lambda comp: flat[
-                    pl.ds(comp * F.shape[1] * pitch + start + at, 8, pitch), :
-                ]
-                real, imag = face(1, 4 + at, part, 1.0 - 2.0 * side, load(near), load(far))
-                YS[side, 0, layer, 8 * part : 8 * part + 8, :] = real
-                YS[side, 1, layer, 8 * part : 8 * part + 8, :] = imag
-
-    with jax.named_scope("faces_z"):
-        @functools.lru_cache(None)
-        def z_edges(comp):
-            packed = None
-            for part in range(cy // 8):
-                rows = slice(LO + 8 * part, LO + 8 * part + 8)
-                for x in range(cx):
-                    spot = part * cx + x
-                    moved = F[comp, 2 + x, rows, :]
-                    if comp == 9:
-                        moved = moved - F[6, 2 + x, rows, :]
-                    if spot:
-                        moved = jnp.where(spot_of == spot, pltpu.roll(moved, 4 * spot, 1), packed)
-                    packed = moved
-            return packed
-
-        @functools.lru_cache(None)
-        def z_near(comp):
-            edges = z_edges(comp)
-            return jnp.where(
-                place == 3, pltpu.roll(edges, 1, 1), jnp.where(place == 0, pltpu.roll(edges, cz - 1, 1), 0.0)
-            )
-
-        sign = jnp.where(place >= 2, 1.0, -1.0)
-        real, imag = face(2, 8, 0, sign, z_near, z_edges)
-        ZS[0] = real
-        ZS[1] = imag
-        real, imag = face(2, 8, 1, sign, z_near, z_edges)
-        POLL[0] = real
-        POLL[1] = imag
-
-    with jax.named_scope("barrier"):
-        pl.semaphore_wait(barrier, sum(count - 1 for _, count, _ in groups))
-
     moves = []
-    for axis, send, recv, send_sem, recv_sem in (
-        ("gx", XS, XR, xs_sem, xr_sem), ("gy", YS, YR, ys_sem, yr_sem), ("gz", ZS, ZR, zs_sem, zr_sem)
-    ):
+
+    def exchange(axis, send, recv, send_sem, recv_sem):
         for side, has, target in ((0, here[axis] > 0, -1), (1, here[axis] < counts[axis] - 1, 1)):
             move = pltpu.make_async_remote_copy(
                 src_ref=send if axis == "gz" else send.at[side],
@@ -459,6 +416,63 @@
             def _(move=move):
                 move.start()
 
+    with jax.named_scope("faces_x"):
+        for at, (side, layer, _, near, far) in enumerate(layers(cx)):
+            for part in range(cy // 8):
+                rows = slice(LO + 8 * part, LO + 8 * part + 8)
+                load = lambda at, rows=rows: None if at is None else lambda comp: F[comp, 2 + at, rows, :]
+                real, imag = face(0, at, part, 1.0 - 2.0 * side, load(near), load(far))
+                XS[side, 0, layer, 8 * part : 8 * part + 8, :] = real
+                XS[side, 1, layer, 8 * part : 8 * part + 8, :] = imag
+    with jax.named_scope("barrier"):
+        pl.semaphore_wait(barrier, sum(group[1] - 1 for group in groups))
+    exchange("gx", XS, XR, xs_sem, xr_sem)
+    with jax.named_scope("faces_z"):
+        packed = {}
+        for part in range(cy // 8):
+            rows = slice(LO + 8 * part, LO + 8 * part + 8)
+            for x in range(cx):
+                spot = part * cx + x
+                mine = spot_of == spot
+                for comp in (3, 5, 1, 2, 4, 7, 8, 9, 10):
+                    moved = F[comp, 2 + x, rows, :]
+                    if comp == 9:
+                        moved = moved - F[6, 2 + x, rows, :]
+                    if spot:
+                        moved = jnp.where(mine, pltpu.roll(moved, 4 * spot, 1), packed[comp])
+                    packed[comp] = moved
+        z_edges = packed.__getitem__
+
+        @functools.lru_cache(None)
+        def z_near(comp):
+            edges = z_edges(comp)
+            return jnp.where(
+                place == 3, pltpu.roll(edges, 1, 1), jnp.where(place == 0, pltpu.roll(edges, cz - 1, 1), 0.0)
+            )
+
+        sign = jnp.where(place >= 2, 1.0, -1.0)
+        real, imag = face(2, 8, 0, sign, z_near, z_edges)
+        ZS[0] = real
+        ZS[1] = imag
+        real, imag = face(2, 8, 1, sign, z_near, z_edges)
+        POLL[0] = real
+        POLL[1] = imag
+    exchange("gz", ZS, ZR, zs_sem, zr_sem)
+    pitch = F.shape[2]
+    flat = F.reshape(12 * F.shape[1] * pitch, cz)
+    with jax.named_scope("faces_y"):
+        for at, (side, layer, _, near, far) in enumerate(layers(cy)):
+            for part in range(cx // 8):
+                start = (2 + 8 * part) * pitch + LO
+                load = lambda at, start=start: None if at is None else lambda comp: flat[
+                    pl.ds(comp * F.shape[1] * pitch + start + at, 8, pitch), :
+                ]
+                real, imag = face(1, 4 + at, part, 1.0 - 2.0 * side, load(near), load(far))
+                YS[side, 0, layer, 8 * part : 8 * part + 8, :] = real
+                YS[side, 1, layer, 8 * part : 8 * part + 8, :] = imag
+
+    exchange("gy", YS, YR, ys_sem, yr_sem)
+
     with jax.named_scope("stencil"):
         @pl.loop(0, cx, unroll=16)
         def _(x_index):
@@ -473,13 +487,8 @@
                 PS[0, x_index, rows : rows + 8, :] = real
                 PS[1, x_index, rows : rows + 8, :] = imag
 
-    with jax.named_scope("harmonics"):
-        for copy in loads[2:6]:
-            copy.wait()
-        ids = ids_ref[...]
-        y_high, y_low = harmonics(*waves(here["gz"], spacing, ids, theta_ref, phi_ref, wave_ref), table_ref[...])
-        sphere = jnp.concatenate([ids[b : b + 1] for b in range(ids.shape[0])], 1) // PTS
-
+    with jax.named_scope("wait_w"):
+        loads[6].wait()
     with jax.named_scope("wait_halo"):
         for has, move, arrival, recv, side in moves:
             @pl.when(has)
@@ -490,21 +499,21 @@
             def _(recv=recv, side=side):
                 recv[side] = jnp.zeros(recv.shape[1:], jnp.float32)
 
+    spread = PS.reshape(2 * cx * cy, cz)
     with jax.named_scope("add_faces"):
         for side in range(2):
             for layer in range(2):
                 x_at, y_at = layer + side * (cx - 2), layer + side * (cy - 2)
                 for c in range(2):
                     PS[c, x_at] = PS[c, x_at] + XR[side, c, layer]
-                    PS[c, :, y_at, :] = PS[c, :, y_at, :] + YR[side, c, layer]
+                    rows = pl.ds(c * cx * cy + y_at, cx, cy)
+                    spread[rows, :] = spread[rows, :] + YR[side, c, layer]
         z_extra = [
             jnp.where(
                 place < 2, pltpu.roll(ZR[1, c] - POLL[c], cz - 2, 1), pltpu.roll(ZR[0, c] - POLL[c], 2, 1)
             )
             for c in range(2)
         ]
-    with jax.named_scope("wait_w"):
-        loads[6].wait()
     with jax.named_scope("swap"):
         rim = (lane < 2) | (lane >= cz - 2)
         width = BLK * BLK
@@ -516,8 +525,7 @@
                     spot = part * cx + x_index
                     extra = pltpu.roll(z_extra[c], cz - 4 * spot, 1) if spot else z_extra[c]
                     parts[c].append(PS[c, x_index, rows : rows + 8, :] + jnp.where(rim, extra, 0.0))
-            for c in range(2):
-                psi_ref[c, x_index] = jnp.concatenate(parts[c], 0).astype(jnp.bfloat16)
+                    PS[c, x_index, rows : rows + 8, :] = parts[c][part]
             for part in range(cy // 8):
                 both = [swap_blocks(parts[c][part]) for c in range(2)]
                 at = x_index * width + part * 8 * BLK
@@ -528,7 +536,7 @@
     with jax.named_scope("project"):
         row = lax.broadcasted_iota(jnp.int32, acc.shape, 0)
         slot = lax.broadcasted_iota(jnp.int32, acc.shape, 1)
-        acc = jnp.where(row % blocks == slot // PB, acc, 0.0)
+        acc = jnp.where(blocks - 1 - row % blocks == slot // PB, acc, 0.0)
         v_re = jnp.sum(acc[:blocks], axis=0, keepdims=True)
         v_im = jnp.sum(acc[blocks:], axis=0, keepdims=True)
         row = lax.broadcasted_iota(jnp.int32, (8, W.shape[0]), 0)
@@ -546,7 +554,7 @@
 
     base = 0
     sends = []
-    for phase, (me, count, peer) in enumerate(groups):
+    for phase, (me, count, peer, rising) in enumerate(groups):
         with jax.named_scope(f"reduce{phase}"):
             MINE[phase] = value
             copies = [
@@ -555,7 +563,7 @@
                     dst_ref=RED.at[base + me],
                     send_sem=ps_sem.at[phase],
                     recv_sem=pr_sem.at[phase],
-                    device_id=peer(step),
+                    device_id=rising(step),
                     device_id_type=LOGICAL,
                 )
                 for step in range(1, count)
@@ -571,6 +579,11 @@
             device_id=peer(1),
             device_id_type=LOGICAL,
         )
+        if phase == 0:
+            with jax.named_scope("store_psi"):
+                for c in range(2):
+                    for x_index in range(cx):
+                        psi_ref[c, x_index] = PS[c, x_index].astype(jnp.bfloat16)
         with jax.named_scope(f"gather{phase}"):
             everything.wait_recv()
             last = phase == len(groups) - 1
@@ -601,14 +614,15 @@
 
 
 def store_kernel(psi_ref, modes_ref, psi_out, modes_out, sem):
-    copies = [
-        pltpu.make_async_copy(psi_ref, psi_out, sem.at[0]),
-        pltpu.make_async_copy(modes_ref, modes_out, sem.at[1]),
-    ]
-    for copy in copies:
-        copy.start()
-    for copy in copies:
-        copy.wait()
+    small = pltpu.make_async_copy(modes_ref, modes_out, sem.at[1])
+    small.start()
+    whole = pltpu.make_async_copy(psi_ref, psi_out, sem.at[0])
+    for c in range(psi_ref.shape[0]):
+        for half in range(2):
+            rows = pl.ds(half * (psi_ref.shape[1] // 2), psi_ref.shape[1] // 2)
+            pltpu.make_async_copy(psi_ref.at[c, rows], psi_out.at[c, rows], sem.at[0]).start()
+    whole.wait()
+    small.wait()
 
 
 def shards(counts, metric_pert, curvature, interp_weights, point_ids, theta, phi):

time: 17.7 us -> 16.5 us (0.932)
  Pallas kernels: 16.9 us -> 15.6 us
    pallas_call x1, Pallas kernels: 16.2 us -> 15 us  [shards(): pl.pallas_call(functools.partial(kernel, counts), out_shape=(pltpu.VMEM((...]
where the time goes in v2:
time: 16.5 us; the launch traced here: 16.3 us
  Pallas kernels  15.6 us (95%)
  between operations  0.64 us (4%)
    pallas_call x1, Pallas kernels, shards(): pl.pallas_call(functools.partial(kernel, counts), out_shape=(pltpu.VMEM((...  15 us
    pallas_call x1, Pallas kernels, shards(): pl.pallas_call(store_kernel, out_shape=(jax.ShapeDtypeStruct(psi.shape, p...  0.67 us

profile of v2, /device:TPU:0, one launch (start us, length us, event | category | flops | bytes accessed | tf_op | source)
XLA Modules:
  0.0 16.3 jit_solution(8859864126868056936)
XLA Ops:
  0.6 15.0 %shard_map.86 = (bf16[2,16,16,128]{3,2,1,0:T(8,128)(2,1)S(1)}, f32[3,2,77]{2,1,0:T(2,128)S(1)}) custom-call(f32[6,16,16,128]{3,2,1,0:T(8,128)} %metric.1, f32[6,16,16,128]{3,2,1,0:T(8,128)} %curvature.1, bf16[512,4096]{1,0:T(8,128)(2,1)} %bitcast.4, s32[8,64]{1,0:T(8,128)} %bitcast.7, f32[48,128]{1,0:T(8,128)} %bitcast.5, f32[48,128]{1,0:T(8,128)} %bitcast.6, ...), custom_call_target="tpu_custom_call" | custom-call | tf_op jit(solution)/shard_map/pallas_call | solution.py:640
  15.6 0.7 %shard_map.87 = (bf16[2,16,16,128]{3,2,1,0:T(8,128)(2,1)}, f32[3,2,77]{2,1,0:T(2,128)}) custom-call(bf16[2,16,16,128]{3,2,1,0:T(8,128)(2,1)S(1)} %get-tuple-element.4.psi_ref, f32[3,2,77]{2,1,0:T(2,128)S(1)} %get-tuple-element.5.modes_ref), custom_call_target="tpu_custom_call" | custom-call | tf_op jit(solution)/shard_map/pallas_call | solution.py:684

commit v3 on v2

--- a/solution.py
+++ b/solution.py
@@ -255,7 +255,7 @@
     spacing = blocks * counts["gz"] // SPHERES
     here = {axis: lax.axis_index(axis) for axis in AXES}
     loads = [
-        pltpu.make_async_copy(source, target, load_sem.at[place])
+        pltpu.make_async_copy(source, target, load_sem.at[max(place - 1, 0)])
         for place, (source, target) in enumerate((
             (metric, F.at[pl.ds(0, 6), pl.ds(2, cx), pl.ds(LO, cy)]),
             (curvature, F.at[pl.ds(6, 6), pl.ds(2, cx), pl.ds(LO, cy)]),
@@ -363,8 +363,8 @@
         sphere = jnp.concatenate([ids[b : b + 1] for b in range(ids.shape[0])], 1) // PTS
 
     with jax.named_scope("wait_fields"):
-        loads[0].wait()
-        loads[1].wait()
+        cells = F.at[pl.ds(0, 12), pl.ds(2, cx), pl.ds(LO, cy)]
+        pltpu.make_async_copy(cells, cells, load_sem.at[0]).wait()
         loads[6].start()
 
     with jax.named_scope("prepare"):
@@ -390,14 +390,15 @@
         weight = tuple(EDGE[n, at, 8 * part : 8 * part + 8, :] for n in range(9))
         return face_tile(axis, weight, laplace, functools.lru_cache(None)(deriv))
 
-    moves = []
+    moves, send_sems = [], []
 
     def exchange(axis, send, recv, send_sem, recv_sem):
+        send_sems.append(send_sem)
         for side, has, target in ((0, here[axis] > 0, -1), (1, here[axis] < counts[axis] - 1, 1)):
             move = pltpu.make_async_remote_copy(
                 src_ref=send if axis == "gz" else send.at[side],
                 dst_ref=recv.at[1 - side],
-                send_sem=send_sem.at[side],
+                send_sem=send_sem.at[0],
                 recv_sem=recv_sem.at[1 - side],
                 device_id={axis: here[axis] + target},
                 device_id_type=MESH,
@@ -405,7 +406,7 @@
             arrival = pltpu.make_async_remote_copy(
                 src_ref=send if axis == "gz" else send.at[side],
                 dst_ref=recv.at[side],
-                send_sem=send_sem.at[side],
+                send_sem=send_sem.at[0],
                 recv_sem=recv_sem.at[side],
                 device_id={axis: here[axis] + target},
                 device_id_type=MESH,
@@ -607,8 +608,18 @@
     with jax.named_scope("tail"):
         for copy in sends:
             copy.wait_send()
-        for has, move, _, _, _ in moves:
-            @pl.when(has)
+        for at in range(0, len(moves), 2):
+            (low, move, _, recv, _), (high, _, _, _, _) = moves[at], moves[at + 1]
+            both = pltpu.make_async_remote_copy(
+                src_ref=recv, dst_ref=recv, send_sem=send_sems[at // 2].at[0], recv_sem=load_sem.at[0],
+                device_id=groups[0][2](1), device_id_type=LOGICAL,
+            )
+
+            @pl.when(jnp.logical_and(low, high))
+            def _(both=both):
+                both.wait_send()
+
+            @pl.when(jnp.logical_xor(low, high))
             def _(move=move):
                 move.wait_send()
 
@@ -666,7 +677,7 @@
             pltpu.VMEM((2, 2, 8, cz), f32),
             pltpu.VMEM((total, HELD, 128), f32),
             pltpu.VMEM((2, HELD, 128), f32),
-            dma((7,)), dma((2,)), dma((2,)), dma((2,)), dma((2,)), dma((2,)), dma((2,)),
+            dma((6,)), dma((1,)), dma((2,)), dma((1,)), dma((2,)), dma((1,)), dma((2,)),
             dma((phases,)), dma((phases,)),
         ],
         compiler_params=pltpu.CompilerParams(

time: 16.5 us -> 16.4 us (level)
  no operation moved by 1% of the time
where the time goes in v3:
time: 16.4 us; the launch traced here: 16.2 us
  Pallas kernels  15.6 us (95%)
  between operations  0.64 us (4%)
    pallas_call x1, Pallas kernels, shards(): pl.pallas_call(functools.partial(kernel, counts), out_shape=(pltpu.VMEM((...  14.9 us
    pallas_call x1, Pallas kernels, shards(): pl.pallas_call(store_kernel, out_shape=(jax.ShapeDtypeStruct(psi.shape, p...  0.67 us

profile of v3, /device:TPU:0, one launch (start us, length us, event | category | flops | bytes accessed | tf_op | source)
XLA Modules:
  0.0 16.2 jit_solution(15334524346530050937)
XLA Ops:
  0.6 14.9 %shard_map.86 = (bf16[2,16,16,128]{3,2,1,0:T(8,128)(2,1)S(1)}, f32[3,2,77]{2,1,0:T(2,128)S(1)}) custom-call(f32[6,16,16,128]{3,2,1,0:T(8,128)} %metric.1, f32[6,16,16,128]{3,2,1,0:T(8,128)} %curvature.1, bf16[512,4096]{1,0:T(8,128)(2,1)} %bitcast.4, s32[8,64]{1,0:T(8,128)} %bitcast.7, f32[48,128]{1,0:T(8,128)} %bitcast.5, f32[48,128]{1,0:T(8,128)} %bitcast.6, ...), custom_call_target="tpu_custom_call" | custom-call | tf_op jit(solution)/shard_map/pallas_call | solution.py:651
  15.6 0.7 %shard_map.87 = (bf16[2,16,16,128]{3,2,1,0:T(8,128)(2,1)}, f32[3,2,77]{2,1,0:T(2,128)}) custom-call(bf16[2,16,16,128]{3,2,1,0:T(8,128)(2,1)S(1)} %get-tuple-element.4.psi_ref, f32[3,2,77]{2,1,0:T(2,128)S(1)} %get-tuple-element.5.modes_ref), custom_call_target="tpu_custom_call" | custom-call | tf_op jit(solution)/shard_map/pallas_call | solution.py:695
